TPU v7x, 256 devices: a whole 4x4x8 slice. The times are simulated.
256 devices in a mesh: macro: 128 (over y, x_lo, z, core), micro: 2 (over x_hi).
Axes of the slice: x: 4 (x_hi: 2, x_lo: 2; x = x_hi * 2 + x_lo), y: 4, z: 8, core: 2. Of those that a mesh axis runs over, the one named last changes fastest.
Arguments:
- macro_state: float32 [65536, 128], P('macro'), may hold values from -6 to 6
- micro_state: bfloat16 [65536, 12, 512], P('macro', None, 'micro'), may hold values from -6 to 6
- velocity: float32 [65536], P('macro'), may hold values from 0.25 to 4
- propagator: bfloat16 [512, 512], P(None, 'micro'), may hold values from -1 to 1
- forcing_map: float32 [128, 512], P(None, 'micro'), may hold values from -0.5 to 0.5
- readout: float32 [128, 512], P(None, 'micro'), may hold values from -1 to 1
- speed_weights: float32 [128], replicated, may hold values from -0.5 to 0.5
Outputs:
- macro_next: float32 [65536, 128], P('macro')
- micro_final: bfloat16 [65536, 12, 512], P('macro', None, 'micro')
All inputs are finite; a program needn't handle non-finite values.
Results may differ from a plain program's by a relative error of at most 0.006.
Values may be sent and summed in bfloat16 or wider, within the bound.
No kernel may reach another device: no remote copies, remote signals or barrier semaphores. Data moves between devices by JAX's collectives and lax.ppermute only.
A program may use at most 64 MiB of HBM per device.

v0:
```python
import jax
import jax.numpy as jnp
from jax import lax
from jax.sharding import Mesh
from jax.sharding import PartitionSpec as P

S = 12
STEPS = 4
MACRO = ("macro_0", "macro_1", "macro_2", "macro_3")


def laid_out(blocks, dim):
    blocks = jnp.moveaxis(blocks, 0, dim)
    dims = blocks.shape
    return blocks.reshape(*dims[:dim], dims[dim] * dims[dim + 1], *dims[dim + 2 :])


def sent_to_all(array, axis):
    copies = jnp.broadcast_to(array, (lax.axis_size(axis), *array.shape))
    return lax.all_to_all(copies, axis, split_axis=0, concat_axis=0, tiled=True)


def gathered_copies(array, axis, dim):
    return laid_out(sent_to_all(array, axis), dim)


def side_by_side(arrays, axis, dim, along):
    widths = [a.shape[along] for a in arrays]
    both = jnp.concatenate(arrays, axis=along)
    result = gathered_copies(both, axis, dim)
    return tuple(jnp.split(result, [sum(widths[:k]) for k in range(1, len(widths))], axis=along))


def taken_together(array, axis):
    everything = sent_to_all(array, axis)
    return jnp.sum(everything.astype(jnp.float32), axis=0)


def cut_along(array, dim, size):
    before, after = (array.shape[:dim], array.shape[dim + 1 :])
    return jnp.moveaxis(array.reshape(*before, size, -1, *after), dim, 0)


def piece_ends(length, count):
    unit = 8 if length >= 8 * count else 1
    return [length // unit * k // count * unit for k in range(1, count)]


def cut_exchange(array, axis, pieces, split_dim, concat_dim):
    blocks = cut_along(array, split_dim, lax.axis_size(axis))
    split_at = max(range(1, max(2, blocks.ndim - 1)), key=lambda d: blocks.shape[d])
    outs = []
    for section in jnp.split(blocks, piece_ends(blocks.shape[split_at], pieces), axis=split_at):
        if section.size:
            outs.append(lax.all_to_all(section, axis, split_axis=0, concat_axis=0, tiled=True))
    return laid_out(jnp.concatenate(outs, axis=split_at), concat_dim)


def by_axis(array, axes):
    for axis in axes:
        array = lax.pmax(array, axis)
    return array


def from_behind(value, axis, steps):
    count = lax.axis_size(axis)
    pairs = [(source, (source + steps) % count) for source in range(count)]
    return lax.ppermute(value, axis, pairs)


def shards(macro_state, micro_state, velocity, propagator, forcing_map, readout, speed_weights):
    highest = lax.Precision.HIGHEST
    coupling = gathered_copies(propagator, "micro", 1)
    forcing_full, readout_full = side_by_side((forcing_map, readout), "micro", 1, 0)
    forcing = jnp.tanh(
        jnp.dot(macro_state, forcing_full, precision=highest, preferred_element_type=jnp.float32)
    )
    micro_now = lax.all_to_all(micro_state, "micro", split_axis=1, concat_axis=2, tiled=True)
    tanh_sum = jnp.zeros(forcing.shape, jnp.float32)
    width = micro_now.shape[2]
    for _ in range(STEPS):
        summed = jnp.dot(micro_now.reshape(-1, width), coupling, preferred_element_type=jnp.float32)
        summed = summed.reshape(micro_now.shape)
        micro_now = (summed + forcing[:, None, :]).astype(jnp.bfloat16)
        tanh_sum = tanh_sum + jnp.sum(jnp.tanh(micro_now.astype(jnp.float32)), axis=1)
    partial_value = jnp.dot(
        tanh_sum / (STEPS * S),
        readout_full.T,
        precision=highest,
        preferred_element_type=jnp.float32,
    )
    forces = taken_together(partial_value.astype(jnp.bfloat16), "micro").astype(jnp.float32)
    micro_final = cut_exchange(micro_now, "micro", 2, 2, 1)
    drive_in = jnp.dot(forces, speed_weights, precision=highest, preferred_element_type=jnp.float32)
    speeds = velocity * (1.5 + jnp.tanh(drive_in))
    fastest = by_axis(jnp.max(speeds), MACRO)
    time_step = 0.8 / jnp.maximum(fastest, 1.0)
    fluxes = speeds[:, None] * macro_state
    stacked = jnp.stack([macro_state, fluxes])
    ahead_rows = from_behind(stacked[:, :1], MACRO, -1)
    state_after = jnp.concatenate([macro_state[1:], ahead_rows[0]], axis=0)
    flux_after = jnp.concatenate([fluxes[1:], ahead_rows[1]], axis=0)
    interface = 0.5 * (fluxes + flux_after) - 0.5 * fastest * (state_after - macro_state)
    carried = from_behind(interface[-1:], MACRO, 1)
    interface_before = jnp.concatenate([carried, interface[:-1]], axis=0)
    macro_next = macro_state - time_step * (interface - interface_before) + time_step * forces
    return (macro_next, micro_final)


def solution(mesh):
    torus = Mesh(
        mesh.devices.reshape(4, 2, 8, 2, mesh.shape["micro"]),
        ("macro_0", "macro_1", "macro_2", "macro_3", "micro"),
    )
    placed = (
        P(MACRO, None),
        P(MACRO, None, "micro"),
        P(MACRO),
        P(None, "micro"),
        P(None, "micro"),
        P(None, "micro"),
        P(),
    )
    return jax.shard_map(
        shards,
        mesh=torus,
        in_specs=placed,
        out_specs=(P(MACRO, None), P(MACRO, None, "micro")),
        check_vma=False,
    )
```

profile of v0, /device:TPU:4, one launch (start us, length us, event | category | flops | bytes accessed | tf_op | source)
XLA Modules:
  0.0 182.2 jit_solution(6250397391435274117)
XLA Ops:
  0.6 0.0 copy-start
  0.6 1.0 pad_maximum_fusion.1
  1.6 0.1 copy.29
  1.8 10.9 %all_to_all.40 = f32[2,256,256]{1,2,0:T(8,128)} all-to-all(f32[2,256,256]{1,2,0:T(8,128)S(1)} %broadcast_in_dim.7), channel_id=1, replica_groups=mesh['macro_0'=4,'macro_1'=2,'macro_2'=8,'macro_3'=2,'micro'=2] {'micro'}, dimensions={0} | all-to-all | bytes 1048576 | tf_op jit(solution)/shard_map/all_to_all | solution.py:20
  12.8 1.0 broadcast_in_dim.6
  13.7 11.1 %all_to_all.41 = bf16[2,512,256]{2,1,0:T(8,128)(2,1)} all-to-all(bf16[2,512,256]{2,1,0:T(8,128)(2,1)S(1)} %broadcast_in_dim.6), channel_id=1, replica_groups=mesh['macro_0'=4,'macro_1'=2,'macro_2'=8,'macro_3'=2,'micro'=2] {'micro'}, dimensions={0} | all-to-all | bytes 1048576 | tf_op jit(solution)/shard_map/all_to_all | solution.py:20
  24.9 7.3 %all-to-all-start = ((bf16[512,12,256]{2,0,1:T(8,128)(2,1)}), bf16[512,12,256]{2,0,1:T(8,128)(2,1)S(1)}, u32[]{:S(2)}, u32[]{:S(2)}) async-start(bf16[512,12,256]{2,0,1:T(8,128)(2,1)} %param.8), calls=%async_computation | async-start | bytes 6291456 | tf_op jit(solution)/shard_map/all_to_all | solution.py:78
  32.1 2.4 %copy.28 = bf16[512,2,256]{2,1,0:T(2,128)(2,1)} copy(bf16[512,2,256]{2,0,1:T(8,128)(2,1)} %bitcast.53) | data formatting | bytes 1048576 | tf_op jit(solution)/shard_map/transpose | solution.py:13
  34.6 2.1 %copy.36 = bf16[512,2,256]{0,2,1:T(8,128)(2,1)} copy(bf16[512,2,256]{2,0,1:T(8,128)(2,1)} %bitcast.54) | data formatting | bytes 1048576 | tf_op jit(solution)/shard_map/reshape | solution.py:15
  36.6 1.8 fusion.18
  38.4 0.0 copy-done.1
  38.4 2.0 %fusion = f32[512,512]{0,1:T(8,128)} fusion(f32[128,512]{0,1:T(8,128)S(1)} %bitcast.60, f32[512,128]{1,0:T(8,128)S(1)} %copy-done.1), kind=kOutput, calls=%fused_computation.12 | convolution fusion | flops 402653184 | bytes 1572864 | tf_op jit(solution)/shard_map/dot_general | solution.py:76
  40.4 2.5 %copy.30 = f32[512,512]{1,0:T(8,128)} copy(f32[512,512]{0,1:T(8,128)} %fusion) | data formatting | bytes 2097152 | tf_op jit(solution)/shard_map/tanh | solution.py:75
  42.9 2.2 %reshape.38 = bf16[512,512,1]{1,0,2:T(8,128)(2,1)} reshape(bf16[512,2,256]{2,1,0:T(2,128)(2,1)} %copy.28) | data formatting | bytes 1048576 | tf_op jit(solution)/shard_map/reshape | solution.py:15
  45.1 18.7 %all-to-all-done = bf16[512,12,256]{2,0,1:T(8,128)(2,1)S(1)} async-done(((bf16[512,12,256]{2,0,1:T(8,128)(2,1)}), bf16[512,12,256]{2,0,1:T(8,128)(2,1)S(1)}, u32[]{:S(2)}, u32[]{:S(2)}) %all-to-all-start) | async-done | bytes 3145760 | tf_op jit(solution)/shard_map/all_to_all | solution.py:78
  63.8 4.9 %copy.42 = bf16[512,2,6,256]{3,1,0,2:T(2,128)(2,1)} copy(bf16[512,2,6,256]{3,0,2,1:T(8,128)(2,1)S(1)} %bitcast.49) | data formatting | bytes 6291456 | tf_op jit(solution)/shard_map/all_to_all | solution.py:78
  68.7 4.6 %dot_general.23 = bf16[512,6,512]{2,0,1:T(8,128)(2,1)S(1)} reshape(bf16[512,6,2,256]{3,2,0,1:T(2,128)(2,1)} %bitcast.51) | data formatting | bytes 6291456 | tf_op jit(solution)/shard_map/dot_general | solution.py:82
  73.3 0.0 copy-start.4
  73.3 0.0 copy-start.7
  73.3 3.8 %tanh_reduce_fusion.3 = (f32[512,512]{1,0:T(8,128)S(1)}, bf16[512,6,512]{2,0,1:T(8,128)(2,1)S(1)}) fusion(f32[512,512]{1,0:T(8,128)} %copy.30, bf16[512,6,512]{2,0,1:T(8,128)(2,1)S(1)} %dot_general.23, bf16[512,512,1]{1,0,2:T(8,128)(2,1)} %reshape.38), kind=kOutput, calls=%fused_computation.6 | convolution fusion | flops 1616642048 | bytes 8912896 | tf_op jit(solution)/shard_map/dot_general | solution.py:82
  77.1 0.0 copy-done.4
  77.1 0.0 copy-done.7
  77.1 2.1 %tanh_reduce_fusion.2 = (f32[512,512]{1,0:T(8,128)S(1)}, bf16[512,6,512]{2,0,1:T(8,128)(2,1)S(1)}) fusion(f32[512,512]{1,0:T(8,128)S(1)} %copy-done.4, bf16[512,6,512]{2,0,1:T(8,128)(2,1)S(1)} %get-tuple-element.17, bf16[512,512,1]{1,0,2:T(8,128)(2,1)S(1)} %copy-done.7), kind=kOutput, calls=%fused_computation.4 | convolution fusion | flops 1616642048 | bytes 8912896 | tf_op jit(solution)/shard_map/dot_general | solution.py:82
  79.2 0.0 copy-start.6
  79.2 2.1 %tanh_reduce_fusion.1 = (f32[512,512]{1,0:T(8,128)S(1)}, bf16[512,6,512]{2,0,1:T(8,128)(2,1)S(1)}) fusion(f32[512,512]{1,0:T(8,128)S(1)} %copy-done.4, bf16[512,6,512]{2,0,1:T(8,128)(2,1)S(1)} %get-tuple-element.19, bf16[512,512,1]{1,0,2:T(8,128)(2,1)S(1)} %copy-done.7), kind=kOutput, calls=%fused_computation.2 | convolution fusion | flops 1616642048 | bytes 8912896 | tf_op jit(solution)/shard_map/dot_general | solution.py:82
  81.3 0.0 copy-done.6
  81.3 0.0 copy-start.5
  81.3 2.1 %tanh_reduce_fusion = (f32[512,512]{1,0:T(8,128)S(1)}, bf16[512,6,512]{2,0,1:T(8,128)(2,1)S(1)}) fusion(f32[512,512]{1,0:T(8,128)S(1)} %copy-done.4, bf16[512,6,512]{2,0,1:T(8,128)(2,1)S(1)} %get-tuple-element.15, bf16[512,512,1]{0,1,2:T(8,128)(2,1)S(1)} %bitcast.61), kind=kOutput, calls=%fused_computation | convolution fusion | flops 1616642048 | bytes 8912896 | tf_op jit(solution)/shard_map/dot_general | solution.py:82
  83.4 0.0 copy-done.5
  83.4 1.0 convolution_convert_fusion
  84.5 0.7 broadcast_in_dim.16
  85.2 7.3 %all-to-all-start.3 = ((bf16[2,512,128]{2,1,0:T(8,128)(2,1)}), bf16[2,512,128]{2,1,0:T(8,128)(2,1)}, u32[]{:S(2)}, u32[]{:S(2)}) async-start(bf16[2,512,128]{2,1,0:T(8,128)(2,1)} %broadcast_in_dim.16), calls=%async_computation.3 | async-start | bytes 524288 | tf_op jit(solution)/shard_map/all_to_all | solution.py:20
  92.5 0.3 copy.41
  92.8 2.0 %fusion.17 = (bf16[2,256,6,256]{3,1,2,0:T(8,128)(2,1)}, bf16[2,256,6,256]{3,1,2,0:T(8,128)(2,1)}) fusion(bf16[2,512,6,256]{3,1,2,0:T(8,128)(2,1)S(1)} %bitcast.50), kind=kLoop, calls=%fused_computation.40 | loop fusion | bytes 6291456 | tf_op jit(solution)/shard_map/split | solution.py:53
  94.8 0.0 copy-start.8
  94.8 1.0 all-to-all-done.3
  95.8 7.2 %all-to-all-start.5 = ((bf16[2,256,6,256]{3,1,2,0:T(8,128)(2,1)}), bf16[2,256,6,256]{3,1,2,0:T(8,128)(2,1)S(1)}, u32[]{:S(2)}, u32[]{:S(2)}) async-start(bf16[2,256,6,256]{3,1,2,0:T(8,128)(2,1)} %get-tuple-element.5), calls=%async_computation.5 | async-start | bytes 3145728 | tf_op jit(solution)/shard_map/all_to_all | solution.py:55
  103.0 1.0 convert_reduce_fusion
  104.0 0.0 copy-start.2
  104.0 0.7 copy-done.2
  104.7 0.0 copy-done
  104.7 0.3 fusion.12
  105.0 0.0 copy-done.8
  105.0 0.6 fusion.16
  105.7 0.9 broadcast_multiply_fusion
  106.6 9.2 %all-to-all-done.5 = bf16[2,256,6,256]{3,1,2,0:T(8,128)(2,1)S(1)} async-done(((bf16[2,256,6,256]{3,1,2,0:T(8,128)(2,1)}), bf16[2,256,6,256]{3,1,2,0:T(8,128)(2,1)S(1)}, u32[]{:S(2)}, u32[]{:S(2)}) %all-to-all-start.5) | async-done | bytes 1572896 | tf_op jit(solution)/shard_map/all_to_all | solution.py:55
  115.8 6.9 %all-to-all-start.4 = ((bf16[2,256,6,256]{3,1,2,0:T(8,128)(2,1)}), bf16[2,256,6,256]{3,1,2,0:T(8,128)(2,1)S(1)}, u32[]{:S(2)}, u32[]{:S(2)}) async-start(bf16[2,256,6,256]{3,1,2,0:T(8,128)(2,1)} %get-tuple-element.4), calls=%async_computation.4 | async-start | bytes 3145728 | tf_op jit(solution)/shard_map/all_to_all | solution.py:55
  122.7 0.7 pad_maximum_fusion.2
  123.4 6.2 %collective-permute-start = (f32[2,1,128]{2,1,0:T(1,128)S(1)}, f32[2,1,128]{2,1,0:T(1,128)S(1)}, u32[]{:S(2)}, u32[]{:S(2)}) collective-permute-start(f32[2,1,128]{2,1,0:T(1,128)S(1)} %pad_maximum_fusion.2), channel_id=1, source_target_pairs={{0,254},{2,0},{4,2},{6,4},{8,6},{10,8},{12,10},{14,12},{16,14},{18... | collective-permute-start | bytes 3080 | tf_op jit(solution)/shard_map/ppermute | solution.py:68
  129.6 9.1 %pmax.28 = f32[]{:T(128)} all-reduce(f32[]{:T(128)} %get-tuple-element.2), channel_id=1, replica_groups=mesh['macro_0'=4,'macro_1'=2,'macro_2'=8,'macro_3'=2,'micro'=2] {'macro_0'}, use_global_device_ids=true, to_apply=%region_6.0 | all-reduce | flops 1 | bytes 8 | tf_op jit(solution)/shard_map/pmax | solution.py:61
  138.6 5.5 %pmax.29 = f32[]{:T(128)} all-reduce(f32[]{:T(128)} %pmax.28), channel_id=1, replica_groups=mesh['macro_0'=4,'macro_1'=2,'macro_2'=8,'macro_3'=2,'micro'=2] {'macro_1'}, use_global_device_ids=true, to_apply=%region_7.0 | all-reduce | flops 1 | bytes 8 | tf_op jit(solution)/shard_map/pmax | solution.py:61
  144.2 19.0 %pmax.30 = f32[]{:T(128)} all-reduce(f32[]{:T(128)} %pmax.29), channel_id=1, replica_groups=mesh['macro_0'=4,'macro_1'=2,'macro_2'=8,'macro_3'=2,'micro'=2] {'macro_2'}, use_global_device_ids=true, to_apply=%region_8.0 | all-reduce | flops 1 | bytes 8 | tf_op jit(solution)/shard_map/pmax | solution.py:61
  163.2 0.7 slice.26
  163.9 3.1 %pmax.31 = f32[]{:T(128)} all-reduce(f32[]{:T(128)} %pmax.30), channel_id=1, replica_groups=mesh['macro_0'=4,'macro_1'=2,'macro_2'=8,'macro_3'=2,'micro'=2] {'macro_3'}, use_global_device_ids=true, to_apply=%region_9.0 | all-reduce | flops 1 | bytes 8 | tf_op jit(solution)/shard_map/pmax | solution.py:61
  167.0 1.7 slice.30
  169.3 0.0 collective-permute-done
  169.3 1.2 fusion.7
  170.5 0.0 copy-start.3
  170.5 0.7 copy-done.3
  171.2 0.2 collective-permute-start.1
  172.0 6.4 %collective-permute-done.1 = f32[1,128]{1,0:T(1,128)S(1)} collective-permute-done((f32[1,128]{1,0:T(1,128)S(1)}, f32[1,128]{1,0:T(1,128)S(1)}, u32[]{:S(2)}, u32[]{:S(2)}) %collective-permute-start.1) | collective-permute-done | bytes 544 | tf_op jit(solution)/shard_map/ppermute | solution.py:68
  178.4 1.9 %fusion.11 = f32[512,128]{1,0:T(8,128)} fusion(f32[512,128]{1,0:T(8,128)S(1)} %copy-done.1, f32[512,128]{1,0:T(8,128)} %copy-done.3, f32[511,128]{1,0:T(8,128)} %bitcast.57, f32[1,128]{1,0:T(1,128)S(1)} %collective-permute-done.1, f32[512,128]{1,0:T(8,128)} %copy-done.2, f32[]{:T(128)S(6)} %div.11), kind=kLoop, calls=%fused_computation.29 | loop fusion | flops 393216 | bytes 1310724 | tf_op jit(solution)/shard_map/add | solution.py:106
  180.3 0.0 all-to-all-done.4
  180.3 1.9 %pad_maximum_fusion = bf16[2,512,6,256]{3,1,2,0:T(8,128)(2,1)} fusion(bf16[2,256,6,256]{3,1,2,0:T(8,128)(2,1)S(1)} %all-to-all-done.5, bf16[2,256,6,256]{3,1,2,0:T(8,128)(2,1)S(1)} %all-to-all-done.4), kind=kLoop, calls=%fused_computation.9 | loop fusion | flops 6291456 | bytes 6291456 | tf_op jit(solution)/shard_map/concatenate | solution.py:56
  (4 shorter events, 0.0 us)
Async XLA Ops:
  0.6 104.1 %copy-start = (f32[128]{0:T(128)S(1)}, f32[128]{0:T(128)}, u32[]{:S(2)}) copy-start(f32[128]{0:T(128)} %param.13) | copy-start | bytes 1540
  24.9 39.0 %all-to-all-start = ((bf16[512,12,256]{2,0,1:T(8,128)(2,1)}), bf16[512,12,256]{2,0,1:T(8,128)(2,1)S(1)}, u32[]{:S(2)}, u32[]{:S(2)}) async-start(bf16[512,12,256]{2,0,1:T(8,128)(2,1)} %param.8), calls=%async_computation | async-start | bytes 6291456 | tf_op jit(solution)/shard_map/all_to_all | solution.py:78
  32.1 6.3 %copy-start.1 = (f32[512,128]{1,0:T(8,128)S(1)}, f32[512,128]{1,0:T(8,128)}, u32[]{:S(2)}) copy-start(f32[512,128]{1,0:T(8,128)} %param.7) | copy-start | bytes 786436
  73.3 3.8 %copy-start.4 = (f32[512,512]{1,0:T(8,128)S(1)}, f32[512,512]{1,0:T(8,128)}, u32[]{:S(2)}) copy-start(f32[512,512]{1,0:T(8,128)} %copy.30) | copy-start | bytes 3145732
  73.3 3.8 %copy-start.7 = (bf16[512,512,1]{1,0,2:T(8,128)(2,1)S(1)}, bf16[512,512,1]{1,0,2:T(8,128)(2,1)}, u32[]{:S(2)}) copy-start(bf16[512,512,1]{1,0,2:T(8,128)(2,1)} %reshape.38) | copy-start | bytes 1572868
  79.2 2.1 %copy-start.6 = (bf16[512,2,256]{0,2,1:T(8,128)(2,1)S(1)}, bf16[512,2,256]{0,2,1:T(8,128)(2,1)}, u32[]{:S(2)}) copy-start(bf16[512,2,256]{0,2,1:T(8,128)(2,1)} %copy.36) | copy-start | bytes 1572868
  81.3 2.1 %copy-start.5 = (f32[128,2,256]{0,2,1:T(8,128)S(1)}, f32[128,2,256]{0,2,1:T(8,128)}, u32[]{:S(2)}) copy-start(f32[128,2,256]{0,2,1:T(8,128)} %get-tuple-element.7) | copy-start | bytes 786436
  85.2 10.6 %all-to-all-start.3 = ((bf16[2,512,128]{2,1,0:T(8,128)(2,1)}), bf16[2,512,128]{2,1,0:T(8,128)(2,1)}, u32[]{:S(2)}, u32[]{:S(2)}) async-start(bf16[2,512,128]{2,1,0:T(8,128)(2,1)} %broadcast_in_dim.16), calls=%async_computation.3 | async-start | bytes 524288 | tf_op jit(solution)/shard_map/all_to_all | solution.py:20
  94.8 10.2 %copy-start.8 = (f32[512]{0:T(512)S(1)}, f32[512]{0:T(512)}, u32[]{:S(2)}) copy-start(f32[512]{0:T(512)} %param.9) | copy-start | bytes 6148
  95.8 20.0 %all-to-all-start.5 = ((bf16[2,256,6,256]{3,1,2,0:T(8,128)(2,1)}), bf16[2,256,6,256]{3,1,2,0:T(8,128)(2,1)S(1)}, u32[]{:S(2)}, u32[]{:S(2)}) async-start(bf16[2,256,6,256]{3,1,2,0:T(8,128)(2,1)} %get-tuple-element.5), calls=%async_computation.5 | async-start | bytes 3145728 | tf_op jit(solution)/shard_map/all_to_all | solution.py:55
  104.0 0.7 copy-start.2
  115.8 64.5 %all-to-all-start.4 = ((bf16[2,256,6,256]{3,1,2,0:T(8,128)(2,1)}), bf16[2,256,6,256]{3,1,2,0:T(8,128)(2,1)S(1)}, u32[]{:S(2)}, u32[]{:S(2)}) async-start(bf16[2,256,6,256]{3,1,2,0:T(8,128)(2,1)} %get-tuple-element.4), calls=%async_computation.4 | async-start | bytes 3145728 | tf_op jit(solution)/shard_map/all_to_all | solution.py:55
  123.4 45.9 %collective-permute-start = (f32[2,1,128]{2,1,0:T(1,128)S(1)}, f32[2,1,128]{2,1,0:T(1,128)S(1)}, u32[]{:S(2)}, u32[]{:S(2)}) collective-permute-start(f32[2,1,128]{2,1,0:T(1,128)S(1)} %pad_maximum_fusion.2), channel_id=1, source_target_pairs={{0,254},{2,0},{4,2},{6,4},{8,6},{10,8},{12,10},{14,12},{16,14},{18... | collective-permute-start | bytes 3080 | tf_op jit(solution)/shard_map/ppermute | solution.py:68
  170.5 0.7 copy-start.3
  171.2 7.2 %collective-permute-start.1 = (f32[1,128]{1,0:T(1,128)S(1)}, f32[1,128]{1,0:T(1,128)S(1)}, u32[]{:S(2)}, u32[]{:S(2)}) collective-permute-start(f32[1,128]{1,0:T(1,128)S(1)} %slice.33), channel_id=1, source_target_pairs={{0,2},{2,4},{4,6},{6,8},{8,10},{10,12},{12,14},{14,16},{16,18},{18... | collective-permute-start | bytes 1544 | tf_op jit(solution)/shard_map/ppermute | solution.py:68
where the time goes:
time: 183 us; the launch traced here: 182 us
  blocking collectives  58.8 us (32%)
  waiting for transfers between devices  35.4 us (19%)
  starting transfers between devices  35 us (19%)
  local copies, waits for them, and re-layouts  28.4 us (16%)
  matrix products  13.4 us (7%)
  other arithmetic  9.2 us (5%)
  between operations  2.04 us (1%)
    pmax x4, blocking collectives, by_axis(): array = lax.pmax(array, axis)  36.7 us
    all_to_all x2, blocking collectives, sent_to_all(): return lax.all_to_all(copies, axis, split_axis=0, concat_axis=0, tiled=True)  22.1 us
    all_to_all x1, waiting for transfers between devices, shards(): lax.all_to_all(micro_state, 'micro', split_axis=1, concat_axis=2, tiled=T...  18.7 us
    all_to_all x2, starting transfers between devices, cut_exchange(): lax.all_to_all(section, axis, split_axis=0, concat_axis=0, tiled=True)  14.1 us
    dot_general x4, matrix products, shards(): jnp.dot(micro_now.reshape(-1, width), coupling, preferred_element_type=jn...  10 us
    all_to_all x2, waiting for transfers between devices, cut_exchange(): lax.all_to_all(section, axis, split_axis=0, concat_axis=0, tiled=True)  9.21 us
    all_to_all x1, starting transfers between devices, sent_to_all(): return lax.all_to_all(copies, axis, split_axis=0, concat_axis=0, tiled=True)  7.32 us
    all_to_all x1, starting transfers between devices, shards(): lax.all_to_all(micro_state, 'micro', split_axis=1, concat_axis=2, tiled=T...  7.27 us
  transfers between devices with their start and end apart: 6, of which 4 were waited for; matrix products, arithmetic and copies ran while one was open for 13% of the time, Pallas kernels for 0%

commit v1 on v0

--- a/solution.py
+++ b/solution.py
@@ -75,7 +75,12 @@
     forcing = jnp.tanh(
         jnp.dot(macro_state, forcing_full, precision=highest, preferred_element_type=jnp.float32)
     )
-    micro_now = lax.all_to_all(micro_state, "micro", split_axis=1, concat_axis=2, tiled=True)
+    micro_now = jnp.concatenate(
+        lax.all_to_all(
+            jnp.stack(jnp.split(micro_state, lax.axis_size("micro"), axis=1)), "micro", 0, 0
+        ),
+        axis=2,
+    )
     tanh_sum = jnp.zeros(forcing.shape, jnp.float32)
     width = micro_now.shape[2]
     for _ in range(STEPS):

time: 183 us -> 177 us (0.967)
  blocking collectives: 58.8 us -> 47.9 us
  starting transfers between devices: 35 us -> 41.5 us
  local copies, waits for them, and re-layouts: 28.4 us -> 23.9 us
  other arithmetic: 9.2 us -> 11.1 us
    all_to_all x2 -> x1, blocking collectives: 22.1 us -> 10.9 us  [sent_to_all(): return lax.all_to_all(copies, axis, split_axis=0, concat_axis=0, tiled=True)]
    all_to_all x1 -> x2, starting transfers between devices: 7.32 us -> 14.1 us  [sent_to_all(): return lax.all_to_all(copies, axis, split_axis=0, concat_axis=0, tiled=True)]
    all_to_all x1 -> x0, local copies, waits for them, and re-layouts: 4.9 us -> none  [shards(): lax.all_to_all(micro_state, 'micro', split_axis=1, concat_axis=2, tiled=T...]
    dot_general x1, local copies, waits for them, and re-layouts: 4.57 us -> 0.27 us  [shards(): jnp.dot(micro_now.reshape(-1, width), coupling, preferred_element_type=jn...]
    another operation x0 -> x1, local copies, waits for them, and re-layouts: none -> 2.08 us  [shards(): jnp.stack(jnp.split(micro_state, lax.axis_size('micro'), axis=1))]
    another operation x0 -> x1, other arithmetic: none -> 1.94 us  [shards(): jnp.stack(jnp.split(micro_state, lax.axis_size('micro'), axis=1))]
    unnamed x18 -> x20, local copies, waits for them, and re-layouts: 1.43 us -> 3.29 us
  transfers between devices with their start and end apart: 6 -> 7, of which waited for: 4 -> 5; matrix products, arithmetic and copies ran while one was open for 13% -> 16% of each run, Pallas kernels for 0% -> 0%
where the time goes in v1:
time: 177 us; the launch traced here: 176 us
  blocking collectives  47.9 us (27%)
  starting transfers between devices  41.5 us (23%)
  waiting for transfers between devices  36.3 us (21%)
  local copies, waits for them, and re-layouts  23.9 us (14%)
  matrix products  12.9 us (7%)
  other arithmetic  11.1 us (6%)
  between operations  2.1 us (1%)
    pmax x4, blocking collectives, by_axis(): array = lax.pmax(array, axis)  37 us
    all_to_all x1, waiting for transfers between devices, shards(): lax.all_to_all(jnp.stack(jnp.split(micro_state, lax.axis_size('micro'), a...  18.7 us
    all_to_all x2, starting transfers between devices, sent_to_all(): return lax.all_to_all(copies, axis, split_axis=0, concat_axis=0, tiled=True)  14.1 us
    all_to_all x2, starting transfers between devices, cut_exchange(): lax.all_to_all(section, axis, split_axis=0, concat_axis=0, tiled=True)  13.9 us
    all_to_all x1, blocking collectives, sent_to_all(): return lax.all_to_all(copies, axis, split_axis=0, concat_axis=0, tiled=True)  10.9 us
    all_to_all x2, waiting for transfers between devices, cut_exchange(): lax.all_to_all(section, axis, split_axis=0, concat_axis=0, tiled=True)  9.47 us
    dot_general x4, matrix products, shards(): jnp.dot(micro_now.reshape(-1, width), coupling, preferred_element_type=jn...  9.44 us
    all_to_all x1, starting transfers between devices, shards(): lax.all_to_all(jnp.stack(jnp.split(micro_state, lax.axis_size('micro'), a...  7.27 us
  transfers between devices with their start and end apart: 7, of which 5 were waited for; matrix products, arithmetic and copies ran while one was open for 16% of the time, Pallas kernels for 0%

profile of v1, /device:TPU:4, one launch (start us, length us, event | category | flops | bytes accessed | tf_op | source)
XLA Modules:
  0.0 175.6 jit_solution(17267120227450437310)
XLA Ops:
  0.6 0.0 copy-start
  0.6 1.0 pad_maximum_fusion.2
  1.6 0.1 copy.29
  1.8 10.9 %all_to_all.30 = f32[2,256,256]{1,2,0:T(8,128)} all-to-all(f32[2,256,256]{1,2,0:T(8,128)S(1)} %broadcast_in_dim.7), channel_id=1, replica_groups=mesh['macro_0'=4,'macro_1'=2,'macro_2'=8,'macro_3'=2,'micro'=2] {'micro'}, dimensions={0} | all-to-all | bytes 1048576 | tf_op jit(solution)/shard_map/all_to_all | solution.py:20
  12.8 1.8 %broadcast_in_dim.6 = bf16[2,512,256]{2,1,0:T(8,128)(2,1)} broadcast(bf16[512,256]{1,0:T(8,128)(2,1)} %param.10), dimensions={1,2} | broadcast | bytes 786432 | tf_op jit(solution)/shard_map/broadcast_in_dim | solution.py:19
  14.5 6.7 %all-to-all-start.1 = ((bf16[2,512,256]{2,1,0:T(8,128)(2,1)}), bf16[2,512,256]{2,1,0:T(8,128)(2,1)S(1)}, u32[]{:S(2)}, u32[]{:S(2)}) async-start(bf16[2,512,256]{2,1,0:T(8,128)(2,1)} %broadcast_in_dim.6), calls=%async_computation.1 | async-start | bytes 1048576 | tf_op jit(solution)/shard_map/all_to_all | solution.py:20
  21.3 2.1 %slice_bitcast_fusion.1 = (bf16[1,512,6,256]{3,1,2,0:T(8,128)(2,1)S(1)}, bf16[1,512,6,256]{3,1,2,0:T(8,128)(2,1)S(1)}) fusion(bf16[512,12,256]{2,0,1:T(8,128)(2,1)} %param.8), kind=kLoop, calls=%fused_computation.12 | loop fusion | bytes 6291456 | tf_op jit(solution)/shard_map/stack | solution.py:80
  23.3 1.9 %pad_maximum_fusion = bf16[2,512,6,256]{3,1,2,0:T(8,128)(2,1)} fusion(bf16[1,512,6,256]{3,1,2,0:T(8,128)(2,1)S(1)} %get-tuple-element.7, bf16[1,512,6,256]{3,1,2,0:T(8,128)(2,1)S(1)} %get-tuple-element.6), kind=kLoop, calls=%fused_computation.9 | loop fusion | flops 1572864 | bytes 6291456 | tf_op jit(solution)/shard_map/stack | solution.py:80
  25.3 0.7 all-to-all-done.1
  26.0 0.8 copy-done.2
  26.8 7.3 %all-to-all-start = ((bf16[2,512,6,256]{3,1,2,0:T(8,128)(2,1)}), bf16[2,512,6,256]{3,1,2,0:T(8,128)(2,1)S(1)}, u32[]{:S(2)}, u32[]{:S(2)}) async-start(bf16[2,512,6,256]{3,1,2,0:T(8,128)(2,1)} %pad_maximum_fusion), calls=%async_computation | async-start | bytes 6291456 | tf_op jit(solution)/shard_map/all_to_all | solution.py:79
  34.1 2.4 %copy.28 = bf16[512,2,256]{2,1,0:T(2,128)(2,1)} copy(bf16[512,2,256]{2,0,1:T(8,128)(2,1)} %bitcast.53) | data formatting | bytes 1048576 | tf_op jit(solution)/shard_map/transpose | solution.py:13
  36.5 2.0 %copy.36 = bf16[512,2,256]{0,2,1:T(8,128)(2,1)} copy(bf16[512,2,256]{2,0,1:T(8,128)(2,1)} %bitcast.54) | data formatting | bytes 1048576 | tf_op jit(solution)/shard_map/reshape | solution.py:15
  38.5 1.8 %fusion.18 = (f32[128,2,256]{0,2,1:T(8,128)S(1)}, f32[128,2,256]{0,2,1:T(8,128)}) fusion(f32[256,2,256]{0,2,1:T(8,128)} %bitcast.59), kind=kLoop, calls=%fused_computation.43 | loop fusion | bytes 1048576 | tf_op jit(solution)/shard_map/split | solution.py:31
  40.3 0.0 copy-done.1
  40.3 2.0 %fusion = f32[512,512]{0,1:T(8,128)} fusion(f32[128,512]{0,1:T(8,128)S(1)} %bitcast.61, f32[512,128]{1,0:T(8,128)S(1)} %copy-done.1), kind=kOutput, calls=%fused_computation.14 | convolution fusion | flops 402653184 | bytes 1572864 | tf_op jit(solution)/shard_map/dot_general | solution.py:76
  42.3 2.5 %copy.30 = f32[512,512]{1,0:T(8,128)} copy(f32[512,512]{0,1:T(8,128)} %fusion) | data formatting | bytes 2097152 | tf_op jit(solution)/shard_map/tanh | solution.py:75
  44.9 2.2 %reshape.40 = bf16[512,512,1]{1,0,2:T(8,128)(2,1)} reshape(bf16[512,2,256]{2,1,0:T(2,128)(2,1)} %copy.28) | data formatting | bytes 1048576 | tf_op jit(solution)/shard_map/reshape | solution.py:15
  47.0 18.7 %all-to-all-done = bf16[2,512,6,256]{3,1,2,0:T(8,128)(2,1)S(1)} async-done(((bf16[2,512,6,256]{3,1,2,0:T(8,128)(2,1)}), bf16[2,512,6,256]{3,1,2,0:T(8,128)(2,1)S(1)}, u32[]{:S(2)}, u32[]{:S(2)}) %all-to-all-start) | async-done | bytes 3145760 | tf_op jit(solution)/shard_map/all_to_all | solution.py:79
  65.8 0.3 copy.39
  66.0 0.9 copy-done.5
  67.0 0.1 copy-done.8
  67.1 2.3 %tanh_reduce_fusion.3 = (f32[512,512]{1,0:T(8,128)S(1)}, bf16[512,6,512]{2,0,1:T(8,128)(2,1)S(1)}) fusion(f32[512,512]{1,0:T(8,128)S(1)} %copy-done.5, bf16[512,6,512]{2,0,1:T(8,128)(2,1)S(1)} %bitcast.57, bf16[512,512,1]{1,0,2:T(8,128)(2,1)S(1)} %copy-done.8), kind=kOutput, calls=%fused_computation.6 | convolution fusion | flops 1616642048 | bytes 8912896 | tf_op jit(solution)/shard_map/dot_general | solution.py:87
  69.5 2.4 %tanh_reduce_fusion.2 = (f32[512,512]{1,0:T(8,128)S(1)}, bf16[512,6,512]{2,0,1:T(8,128)(2,1)S(1)}) fusion(f32[512,512]{1,0:T(8,128)S(1)} %copy-done.5, bf16[512,6,512]{2,0,1:T(8,128)(2,1)S(1)} %get-tuple-element.19, bf16[512,512,1]{1,0,2:T(8,128)(2,1)S(1)} %copy-done.8), kind=kOutput, calls=%fused_computation.4 | convolution fusion | flops 1616642048 | bytes 8912896 | tf_op jit(solution)/shard_map/dot_general | solution.py:87
  71.8 0.0 copy-start.7
  71.9 2.3 %tanh_reduce_fusion.1 = (f32[512,512]{1,0:T(8,128)S(1)}, bf16[512,6,512]{2,0,1:T(8,128)(2,1)S(1)}) fusion(f32[512,512]{1,0:T(8,128)S(1)} %copy-done.5, bf16[512,6,512]{2,0,1:T(8,128)(2,1)S(1)} %get-tuple-element.21, bf16[512,512,1]{1,0,2:T(8,128)(2,1)S(1)} %copy-done.8), kind=kOutput, calls=%fused_computation.2 | convolution fusion | flops 1616642048 | bytes 8912896 | tf_op jit(solution)/shard_map/dot_general | solution.py:87
  74.2 0.0 copy-done.7
  74.2 0.0 copy-start.6
  74.2 2.4 %tanh_reduce_fusion = (f32[512,512]{1,0:T(8,128)S(1)}, bf16[512,6,512]{2,0,1:T(8,128)(2,1)S(1)}) fusion(f32[512,512]{1,0:T(8,128)S(1)} %copy-done.5, bf16[512,6,512]{2,0,1:T(8,128)(2,1)S(1)} %get-tuple-element.17, bf16[512,512,1]{0,1,2:T(8,128)(2,1)S(1)} %bitcast.62), kind=kOutput, calls=%fused_computation | convolution fusion | flops 1616642048 | bytes 8912896 | tf_op jit(solution)/shard_map/dot_general | solution.py:87
  76.6 0.0 copy-done.6
  76.6 1.1 convolution_convert_fusion
  77.7 0.7 broadcast_in_dim.16
  78.5 7.3 %all-to-all-start.3 = ((bf16[2,512,128]{2,1,0:T(8,128)(2,1)}), bf16[2,512,128]{2,1,0:T(8,128)(2,1)}, u32[]{:S(2)}, u32[]{:S(2)}) async-start(bf16[2,512,128]{2,1,0:T(8,128)(2,1)} %broadcast_in_dim.16), calls=%async_computation.3 | async-start | bytes 524288 | tf_op jit(solution)/shard_map/all_to_all | solution.py:20
  85.8 0.3 copy.41
  86.1 2.0 %fusion.17 = (bf16[2,256,6,256]{3,1,2,0:T(8,128)(2,1)}, bf16[2,256,6,256]{3,1,2,0:T(8,128)(2,1)}) fusion(bf16[2,512,6,256]{3,1,2,0:T(8,128)(2,1)S(1)} %bitcast.51), kind=kLoop, calls=%fused_computation.42 | loop fusion | bytes 6291456 | tf_op jit(solution)/shard_map/split | solution.py:53
  88.1 1.0 all-to-all-done.3
  89.1 7.2 %all-to-all-start.5 = ((bf16[2,256,6,256]{3,1,2,0:T(8,128)(2,1)}), bf16[2,256,6,256]{3,1,2,0:T(8,128)(2,1)S(1)}, u32[]{:S(2)}, u32[]{:S(2)}) async-start(bf16[2,256,6,256]{3,1,2,0:T(8,128)(2,1)} %get-tuple-element.5), calls=%async_computation.5 | async-start | bytes 3145728 | tf_op jit(solution)/shard_map/all_to_all | solution.py:55
  96.3 1.0 convert_reduce_fusion
  97.3 0.0 copy-start.3
  97.3 0.7 copy-done.3
  98.0 0.0 copy-done
  98.0 0.3 fusion.12
  98.3 0.0 copy-done.9
  98.3 0.6 fusion.16
  98.9 0.9 broadcast_multiply_fusion
  99.8 9.5 %all-to-all-done.5 = bf16[2,256,6,256]{3,1,2,0:T(8,128)(2,1)S(1)} async-done(((bf16[2,256,6,256]{3,1,2,0:T(8,128)(2,1)}), bf16[2,256,6,256]{3,1,2,0:T(8,128)(2,1)S(1)}, u32[]{:S(2)}, u32[]{:S(2)}) %all-to-all-start.5) | async-done | bytes 1572896 | tf_op jit(solution)/shard_map/all_to_all | solution.py:55
  109.3 6.7 %all-to-all-start.4 = ((bf16[2,256,6,256]{3,1,2,0:T(8,128)(2,1)}), bf16[2,256,6,256]{3,1,2,0:T(8,128)(2,1)S(1)}, u32[]{:S(2)}, u32[]{:S(2)}) async-start(bf16[2,256,6,256]{3,1,2,0:T(8,128)(2,1)} %get-tuple-element.4), calls=%async_computation.4 | async-start | bytes 3145728 | tf_op jit(solution)/shard_map/all_to_all | solution.py:55
  116.0 0.7 pad_maximum_fusion.3
  116.7 6.1 %collective-permute-start = (f32[2,1,128]{2,1,0:T(1,128)S(1)}, f32[2,1,128]{2,1,0:T(1,128)S(1)}, u32[]{:S(2)}, u32[]{:S(2)}) collective-permute-start(f32[2,1,128]{2,1,0:T(1,128)S(1)} %pad_maximum_fusion.3), channel_id=1, source_target_pairs={{0,254},{2,0},{4,2},{6,4},{8,6},{10,8},{12,10},{14,12},{16,14},{18... | collective-permute-start | bytes 3080 | tf_op jit(solution)/shard_map/ppermute | solution.py:68
  122.8 9.1 %pmax.28 = f32[]{:T(128)} all-reduce(f32[]{:T(128)} %get-tuple-element.2), channel_id=1, replica_groups=mesh['macro_0'=4,'macro_1'=2,'macro_2'=8,'macro_3'=2,'micro'=2] {'macro_0'}, use_global_device_ids=true, to_apply=%region_6.0 | all-reduce | flops 1 | bytes 8 | tf_op jit(solution)/shard_map/pmax | solution.py:61
  131.9 5.6 %pmax.29 = f32[]{:T(128)} all-reduce(f32[]{:T(128)} %pmax.28), channel_id=1, replica_groups=mesh['macro_0'=4,'macro_1'=2,'macro_2'=8,'macro_3'=2,'micro'=2] {'macro_1'}, use_global_device_ids=true, to_apply=%region_7.0 | all-reduce | flops 1 | bytes 8 | tf_op jit(solution)/shard_map/pmax | solution.py:61
  137.5 19.1 %pmax.30 = f32[]{:T(128)} all-reduce(f32[]{:T(128)} %pmax.29), channel_id=1, replica_groups=mesh['macro_0'=4,'macro_1'=2,'macro_2'=8,'macro_3'=2,'micro'=2] {'macro_2'}, use_global_device_ids=true, to_apply=%region_8.0 | all-reduce | flops 1 | bytes 8 | tf_op jit(solution)/shard_map/pmax | solution.py:61
  156.6 0.7 slice.26
  157.3 3.1 %pmax.31 = f32[]{:T(128)} all-reduce(f32[]{:T(128)} %pmax.30), channel_id=1, replica_groups=mesh['macro_0'=4,'macro_1'=2,'macro_2'=8,'macro_3'=2,'micro'=2] {'macro_3'}, use_global_device_ids=true, to_apply=%region_9.0 | all-reduce | flops 1 | bytes 8 | tf_op jit(solution)/shard_map/pmax | solution.py:61
  160.4 1.7 slice.30
  162.7 0.0 collective-permute-done
  162.8 1.2 fusion.7
  163.9 0.0 copy-start.4
  164.0 0.7 copy-done.4
  164.7 0.2 collective-permute-start.1
  165.5 6.4 %collective-permute-done.1 = f32[1,128]{1,0:T(1,128)S(1)} collective-permute-done((f32[1,128]{1,0:T(1,128)S(1)}, f32[1,128]{1,0:T(1,128)S(1)}, u32[]{:S(2)}, u32[]{:S(2)}) %collective-permute-start.1) | collective-permute-done | bytes 544 | tf_op jit(solution)/shard_map/ppermute | solution.py:68
  171.9 1.9 %fusion.11 = f32[512,128]{1,0:T(8,128)} fusion(f32[512,128]{1,0:T(8,128)S(1)} %copy-done.1, f32[512,128]{1,0:T(8,128)} %copy-done.4, f32[511,128]{1,0:T(8,128)} %bitcast.58, f32[1,128]{1,0:T(1,128)S(1)} %collective-permute-done.1, f32[512,128]{1,0:T(8,128)} %copy-done.3, f32[]{:T(128)S(6)} %div.11), kind=kLoop, calls=%fused_computation.31 | loop fusion | flops 393216 | bytes 1310724 | tf_op jit(solution)/shard_map/add | solution.py:111
  173.8 0.0 all-to-all-done.4
  173.8 1.9 %pad_maximum_fusion.1 = bf16[2,512,6,256]{3,1,2,0:T(8,128)(2,1)} fusion(bf16[2,256,6,256]{3,1,2,0:T(8,128)(2,1)S(1)} %all-to-all-done.5, bf16[2,256,6,256]{3,1,2,0:T(8,128)(2,1)S(1)} %all-to-all-done.4), kind=kLoop, calls=%fused_computation.10 | loop fusion | flops 6291456 | bytes 6291456 | tf_op jit(solution)/shard_map/concatenate | solution.py:56
  (8 shorter events, 0.1 us)
Async XLA Ops:
  0.6 97.3 %copy-start = (f32[128]{0:T(128)S(1)}, f32[128]{0:T(128)}, u32[]{:S(2)}) copy-start(f32[128]{0:T(128)} %param.13) | copy-start | bytes 1540
  14.5 11.5 %all-to-all-start.1 = ((bf16[2,512,256]{2,1,0:T(8,128)(2,1)}), bf16[2,512,256]{2,1,0:T(8,128)(2,1)S(1)}, u32[]{:S(2)}, u32[]{:S(2)}) async-start(bf16[2,512,256]{2,1,0:T(8,128)(2,1)} %broadcast_in_dim.6), calls=%async_computation.1 | async-start | bytes 1048576 | tf_op jit(solution)/shard_map/all_to_all | solution.py:20
  26.0 0.8 copy-start.2
  26.8 39.0 %all-to-all-start = ((bf16[2,512,6,256]{3,1,2,0:T(8,128)(2,1)}), bf16[2,512,6,256]{3,1,2,0:T(8,128)(2,1)S(1)}, u32[]{:S(2)}, u32[]{:S(2)}) async-start(bf16[2,512,6,256]{3,1,2,0:T(8,128)(2,1)} %pad_maximum_fusion), calls=%async_computation | async-start | bytes 6291456 | tf_op jit(solution)/shard_map/all_to_all | solution.py:79
  34.1 6.2 %copy-start.1 = (f32[512,128]{1,0:T(8,128)S(1)}, f32[512,128]{1,0:T(8,128)}, u32[]{:S(2)}) copy-start(f32[512,128]{1,0:T(8,128)} %param.7) | copy-start | bytes 786436
  65.8 1.2 copy-start.5
  65.8 1.4 copy-start.8
  71.8 2.4 %copy-start.7 = (bf16[512,2,256]{0,2,1:T(8,128)(2,1)S(1)}, bf16[512,2,256]{0,2,1:T(8,128)(2,1)}, u32[]{:S(2)}) copy-start(bf16[512,2,256]{0,2,1:T(8,128)(2,1)} %copy.36) | copy-start | bytes 1572868
  74.2 2.4 %copy-start.6 = (f32[128,2,256]{0,2,1:T(8,128)S(1)}, f32[128,2,256]{0,2,1:T(8,128)}, u32[]{:S(2)}) copy-start(f32[128,2,256]{0,2,1:T(8,128)} %get-tuple-element.9) | copy-start | bytes 786436
  78.5 10.6 %all-to-all-start.3 = ((bf16[2,512,128]{2,1,0:T(8,128)(2,1)}), bf16[2,512,128]{2,1,0:T(8,128)(2,1)}, u32[]{:S(2)}, u32[]{:S(2)}) async-start(bf16[2,512,128]{2,1,0:T(8,128)(2,1)} %broadcast_in_dim.16), calls=%async_computation.3 | async-start | bytes 524288 | tf_op jit(solution)/shard_map/all_to_all | solution.py:20
  88.1 10.2 %copy-start.9 = (f32[512]{0:T(512)S(1)}, f32[512]{0:T(512)}, u32[]{:S(2)}) copy-start(f32[512]{0:T(512)} %param.9) | copy-start | bytes 6148
  89.1 20.2 %all-to-all-start.5 = ((bf16[2,256,6,256]{3,1,2,0:T(8,128)(2,1)}), bf16[2,256,6,256]{3,1,2,0:T(8,128)(2,1)S(1)}, u32[]{:S(2)}, u32[]{:S(2)}) async-start(bf16[2,256,6,256]{3,1,2,0:T(8,128)(2,1)} %get-tuple-element.5), calls=%async_computation.5 | async-start | bytes 3145728 | tf_op jit(solution)/shard_map/all_to_all | solution.py:55
  97.3 0.7 copy-start.3
  109.3 64.5 %all-to-all-start.4 = ((bf16[2,256,6,256]{3,1,2,0:T(8,128)(2,1)}), bf16[2,256,6,256]{3,1,2,0:T(8,128)(2,1)S(1)}, u32[]{:S(2)}, u32[]{:S(2)}) async-start(bf16[2,256,6,256]{3,1,2,0:T(8,128)(2,1)} %get-tuple-element.4), calls=%async_computation.4 | async-start | bytes 3145728 | tf_op jit(solution)/shard_map/all_to_all | solution.py:55
  116.7 46.1 %collective-permute-start = (f32[2,1,128]{2,1,0:T(1,128)S(1)}, f32[2,1,128]{2,1,0:T(1,128)S(1)}, u32[]{:S(2)}, u32[]{:S(2)}) collective-permute-start(f32[2,1,128]{2,1,0:T(1,128)S(1)} %pad_maximum_fusion.3), channel_id=1, source_target_pairs={{0,254},{2,0},{4,2},{6,4},{8,6},{10,8},{12,10},{14,12},{16,14},{18... | collective-permute-start | bytes 3080 | tf_op jit(solution)/shard_map/ppermute | solution.py:68
  163.9 0.7 copy-start.4
  164.7 7.2 %collective-permute-start.1 = (f32[1,128]{1,0:T(1,128)S(1)}, f32[1,128]{1,0:T(1,128)S(1)}, u32[]{:S(2)}, u32[]{:S(2)}) collective-permute-start(f32[1,128]{1,0:T(1,128)S(1)} %slice.33), channel_id=1, source_target_pairs={{0,2},{2,4},{4,6},{6,8},{8,10},{10,12},{12,14},{14,16},{16,18},{18... | collective-permute-start | bytes 1544 | tf_op jit(solution)/shard_map/ppermute | solution.py:68
